TPU v7x, 256 devices: a whole 4x4x8 slice. The times are simulated.
256 devices in a mesh: dp: 32 (over z, y_hi, core), tensor: 8 (over x, y_lo).
Axes of the slice: x: 4, y: 4 (y_hi: 2, y_lo: 2; y = y_hi * 2 + y_lo), z: 8, core: 2. Of those that a mesh axis runs over, the one named last changes fastest.
Arguments:
- tokens: bfloat16 [128, 576, 1024], P('dp', 'tensor'), may hold values from -150 to 150
- cotangent: bfloat16 [128, 576, 1024], P('dp', 'tensor'), may hold values from -6 to 6
- dispatch_weight: bfloat16 [1024, 64], replicated, may hold values from -3 to 3
- w_in: bfloat16 [64, 1024, 4096], P('dp', None, 'tensor'), may hold values from -0.1875 to 0.1875
- w_out: bfloat16 [64, 4096, 1024], P('dp', 'tensor'), may hold values from -0.09375 to 0.09375
Outputs:
- grad_tokens: bfloat16 [128, 576, 1024], P('dp', 'tensor')
- grad_router: float32 [1024, 64], replicated
- grad_w_in: bfloat16 [64, 1024, 4096], P('dp', None, 'tensor')
- grad_w_out: bfloat16 [64, 4096, 1024], P('dp', 'tensor')
All inputs are finite; a program needn't handle non-finite values.
Results may differ from a plain program's by a relative error of at most 0.0079.
Values may be sent and summed in bfloat16 or wider, within the bound.
A program may use at most 64 MiB of HBM per device.

v0:
```python
import jax
import jax.numpy as jnp
from jax import lax
from jax.sharding import PartitionSpec as P


def split_up(x, dim, length):
    lengths = x.shape
    blocks = x.reshape(*lengths[:dim], length, lengths[dim] // length, *lengths[dim + 1 :])
    return jnp.moveaxis(blocks, dim, 0)


def summed_on_arrival(x, axis, dim):
    blocks = split_up(x, dim, lax.axis_size(axis))
    arrived = lax.all_to_all(blocks, axis, split_axis=0, concat_axis=0, tiled=True)
    return arrived.sum(axis=0)


def sent_to_all(x, axis):
    length = lax.axis_size(axis)
    return lax.all_to_all(jnp.broadcast_to(x[None], (length, *x.shape)), axis, 0, 0, tiled=True)


def laid_out(blocks, dim):
    lengths = list(blocks.shape[1:])
    lengths[dim] *= blocks.shape[0]
    return jnp.moveaxis(blocks, 0, dim).reshape(lengths)


def gathered_copies(x, axis, dim):
    blocks = sent_to_all(x, axis)
    return laid_out(blocks, dim)


def collected_together(x, axis):
    leaves = jax.tree.leaves(x)
    sequence = sorted(range(len(leaves)), key=lambda k: -leaves[k].size)
    width = (1, *leaves[sequence[0]].shape)[-1]
    lines = [
        jnp.pad(leaves[k].reshape(-1), (0, -leaves[k].size % width)).reshape(-1, width)
        for k in sequence
    ]
    both, at, found = (sent_to_all(jnp.concatenate(lines), axis), 0, {})
    for k, line in zip(sequence, lines):
        piece = both[:, at : at + len(line)].reshape(len(both), -1)
        found[k] = piece[:, : leaves[k].size].reshape(-1, *leaves[k].shape)
        at += len(line)
    numbers = iter(range(len(leaves)))
    return jax.tree.map(lambda _: found[next(numbers)], x)


def combined_pairwise(pieces, combine):
    while len(jax.tree.leaves(pieces)[0]) > 1:
        pieces = jax.vmap(combine)(
            *(jax.tree.map(lambda part: part[side::2], pieces) for side in (0, 1))
        )
    return jax.tree.map(lambda part: part[0], pieces)


def merged(x, axis, combine):
    pieces = collected_together(x, axis)
    return combined_pairwise(pieces, combine)


def over_copies(x, axis):
    return sent_to_all(x, axis).sum(axis=0)


def to_experts(partial_rows):
    shared_part = summed_on_arrival(partial_rows, "tensor", 2).astype(jnp.bfloat16)
    arrived = lax.all_to_all(shared_part, "dp", split_axis=1, concat_axis=0, tiled=True)
    result = gathered_copies(arrived, "tensor", 2)
    return result


def to_images(partial_rows):
    shared_part = summed_on_arrival(partial_rows, "tensor", 2).astype(jnp.bfloat16)
    arrived = lax.all_to_all(shared_part, "dp", split_axis=0, concat_axis=1, tiled=True)
    result = gathered_copies(arrived, "tensor", 2)
    return result


def join_stats(former, latter):
    biggest = jnp.maximum(former[0], latter[0])
    return (
        biggest,
        former[1] * jnp.exp(former[0] - biggest) + latter[1] * jnp.exp(latter[0] - biggest),
    )


def dispatch_softmax(logits):
    local_max = jnp.max(logits, axis=1)
    local_total = jnp.sum(jnp.exp(logits - local_max[:, None, :]), axis=1)
    global_max, totals = merged((local_max, local_total), "tensor", join_stats)
    exponent = jnp.exp(logits - global_max[:, None, :])
    return exponent / totals[:, None, :]


def on_device(tokens, cotangent, dispatch_weight, w_in, w_out):
    wide = jnp.float32
    logits = jnp.einsum("isd,de->ise", tokens, dispatch_weight, preferred_element_type=wide)
    dispatch = dispatch_softmax(logits)
    combine = jax.nn.softmax(logits, axis=2)
    dispatch_low = dispatch.astype(jnp.bfloat16)
    combine_low = combine.astype(jnp.bfloat16)
    slot_inputs = to_experts(
        jnp.einsum("ise,isd->ied", dispatch_low, tokens, preferred_element_type=wide)
    )
    pre_act = jnp.einsum("ied,edf->ief", slot_inputs, w_in, preferred_element_type=wide)
    hidden_act, gelu_back = jax.vjp(jax.nn.gelu, pre_act)
    hidden_low = hidden_act.astype(jnp.bfloat16)
    slot_outputs = to_images(
        jnp.einsum("ief,efd->ied", hidden_low, w_out, preferred_element_type=wide)
    )
    grad_combine = jnp.einsum("isd,ied->ise", cotangent, slot_outputs, preferred_element_type=wide)
    grad_slots_out = to_experts(
        jnp.einsum("ise,isd->ied", combine_low, cotangent, preferred_element_type=wide)
    )
    grad_hidden = jnp.einsum("ied,efd->ief", grad_slots_out, w_out, preferred_element_type=wide)
    grad_pre = gelu_back(grad_hidden)[0].astype(jnp.bfloat16)
    grad_w_out = jnp.einsum(
        "ief,ied->efd", hidden_low, grad_slots_out, preferred_element_type=wide
    ).astype(jnp.bfloat16)
    grad_w_in = jnp.einsum(
        "ied,ief->edf", slot_inputs, grad_pre, preferred_element_type=wide
    ).astype(jnp.bfloat16)
    grad_slots_in = to_images(
        jnp.einsum("ief,edf->ied", grad_pre, w_in, preferred_element_type=wide)
    )
    grad_dispatch = jnp.einsum("isd,ied->ise", tokens, grad_slots_in, preferred_element_type=wide)
    column_dot = over_copies(jnp.sum(grad_dispatch * dispatch, axis=1), "tensor")
    row_dot = jnp.sum(grad_combine * combine, axis=2, keepdims=True)
    grad_logits = (
        combine * (grad_combine - row_dot) + dispatch * (grad_dispatch - column_dot[:, None, :])
    ).astype(jnp.bfloat16)
    token_part = jnp.einsum(
        "ise,ied->isd", dispatch_low, grad_slots_in, preferred_element_type=wide
    )
    router_part = jnp.einsum(
        "ise,de->isd", grad_logits, dispatch_weight, preferred_element_type=wide
    )
    grad_tokens = (token_part + router_part).astype(jnp.bfloat16)
    local_router = jnp.einsum("isd,ise->de", tokens, grad_logits, preferred_element_type=wide)
    grad_router = lax.psum(local_router, ("dp", "tensor"))
    return (grad_tokens, grad_router, grad_w_in, grad_w_out)


def solution(mesh):
    return jax.shard_map(
        on_device,
        mesh=mesh,
        in_specs=(
            P("dp", "tensor", None),
            P("dp", "tensor", None),
            P(),
            P("dp", None, "tensor"),
            P("dp", "tensor", None),
        ),
        out_specs=(P("dp", "tensor", None), P(), P("dp", None, "tensor"), P("dp", "tensor", None)),
        check_vma=False,
    )
```

profile of v0, /device:TPU:2, one launch (start us, length us, event | category | flops | bytes accessed | tf_op | source)
XLA Modules:
  0.0 496.0 jit_solution(7292811887007530040)
XLA Ops:
  7.2 1.7 fusion.48
  9.2 10.4 %all_to_all.110 = f32[8,1,512]{2,1,0:T(1,128)S(1)} all-to-all(f32[8,1,512]{2,1,0:T(1,128)S(1)} %reshape.63), channel_id=1, replica_groups=mesh['dp'=32,'tensor'=8] {'tensor'}, dimensions={0} | all-to-all | bytes 32768 | tf_op jit(solution)/shard_map/all_to_all | solution.py:21
  20.9 1.4 convolution_bitcast_fusion.2
  22.3 1.1 copy.151
  23.4 5.6 %all-to-all-start.4 = ((f32[8,4,64,128]{3,2,1,0:T(8,128)}), f32[8,4,64,128]{3,2,1,0:T(8,128)}, u32[]{:S(2)}, u32[]{:S(2)}) async-start(f32[8,4,64,128]{3,2,1,0:T(8,128)} %bitcast.137), calls=%async_computation.4 | async-start | bytes 2097152 | tf_op jit(solution)/shard_map/all_to_all | solution.py:15
  29.0 0.7 fusion.49
  29.7 1.4 convolution_bitcast_fusion.3
  31.0 1.1 copy.152
  32.1 9.9 %all-to-all-done.4 = f32[8,4,64,128]{3,2,1,0:T(8,128)} async-done(((f32[8,4,64,128]{3,2,1,0:T(8,128)}), f32[8,4,64,128]{3,2,1,0:T(8,128)}, u32[]{:S(2)}, u32[]{:S(2)}) %all-to-all-start.4) | async-done | bytes 1048608 | tf_op jit(solution)/shard_map/all_to_all | solution.py:15
  42.1 4.9 all-to-all-start.1
  47.0 1.3 reduce_sum.84
  48.3 0.7 copy.87
  49.0 11.1 %all-to-all-done.1 = f32[8,4,64,128]{3,2,1,0:T(8,128)S(1)} async-done(((f32[8,4,64,128]{3,2,1,0:T(8,128)}), f32[8,4,64,128]{3,2,1,0:T(8,128)S(1)}, u32[]{:S(2)}, u32[]{:S(2)}) %all-to-all-start.1) | async-done | bytes 1048608 | tf_op jit(solution)/shard_map/all_to_all | solution.py:15
  60.1 11.2 %all-to-all-start.5 = ((bf16[4,64,128]{2,0,1:T(4,128)(2,1)}), bf16[4,64,128]{2,0,1:T(4,128)(2,1)S(1)}, u32[]{:S(2)}, u32[]{:S(2)}) async-start(bf16[4,64,128]{2,0,1:T(4,128)(2,1)} %copy.87), calls=%async_computation.5 | async-start | bytes 131072 | tf_op jit(solution)/shard_map/all_to_all | solution.py:71
  71.3 0.7 copy.82
  72.0 9.2 %all-to-all-done.5 = bf16[4,64,128]{2,0,1:T(4,128)(2,1)S(1)} async-done(((bf16[4,64,128]{2,0,1:T(4,128)(2,1)}), bf16[4,64,128]{2,0,1:T(4,128)(2,1)S(1)}, u32[]{:S(2)}, u32[]{:S(2)}) %all-to-all-start.5) | async-done | bytes 65568 | tf_op jit(solution)/shard_map/all_to_all | solution.py:71
  81.2 3.9 all-to-all-start.2
  85.2 9.9 %all-to-all-done.2 = bf16[4,64,128]{2,0,1:T(4,128)(2,1)S(1)} async-done(((bf16[4,64,128]{2,0,1:T(4,128)(2,1)}), bf16[4,64,128]{2,0,1:T(4,128)(2,1)S(1)}, u32[]{:S(2)}, u32[]{:S(2)}) %all-to-all-start.2) | async-done | bytes 65568 | tf_op jit(solution)/shard_map/all_to_all | solution.py:71
  95.0 0.9 broadcast_in_dim.24
  95.9 4.9 all-to-all-start.6
  100.9 8.5 %all-to-all-done.6 = bf16[8,128,2,128]{3,1,2,0:T(8,128)(2,1)S(1)} async-done(((bf16[8,128,2,128]{3,1,2,0:T(8,128)(2,1)}), bf16[8,128,2,128]{3,1,2,0:T(8,128)(2,1)S(1)}, u32[]{:S(2)}, u32[]{:S(2)}) %all-to-all-start.6) | async-done | bytes 524320 | tf_op jit(solution)/shard_map/all_to_all | solution.py:21
  109.4 0.9 broadcast_in_dim.22
  110.3 5.5 %all-to-all-start.3 = ((bf16[8,128,2,128]{3,1,2,0:T(8,128)(2,1)}), bf16[8,128,2,128]{3,1,2,0:T(8,128)(2,1)}, u32[]{:S(2)}, u32[]{:S(2)}) async-start(bf16[8,128,2,128]{3,1,2,0:T(8,128)(2,1)} %broadcast_in_dim.22), calls=%async_computation.3 | async-start | bytes 1048576 | tf_op jit(solution)/shard_map/all_to_all | solution.py:21
  116.2 7.5 %all-to-all-done.3 = bf16[8,128,2,128]{3,1,2,0:T(8,128)(2,1)} async-done(((bf16[8,128,2,128]{3,1,2,0:T(8,128)(2,1)}), bf16[8,128,2,128]{3,1,2,0:T(8,128)(2,1)}, u32[]{:S(2)}, u32[]{:S(2)}) %all-to-all-start.3) | async-done | bytes 524320 | tf_op jit(solution)/shard_map/all_to_all | solution.py:21
  123.7 2.8 fusion.15
  126.5 0.8 convolution_bitcast_fusion.1
  127.3 1.1 copy.150
  128.3 5.5 %all-to-all-start.7 = ((f32[8,128,2,128]{3,1,2,0:T(8,128)}), f32[8,128,2,128]{3,1,2,0:T(8,128)}, u32[]{:S(2)}, u32[]{:S(2)}) async-start(f32[8,128,2,128]{3,1,2,0:T(8,128)} %bitcast.142), calls=%async_computation.7 | async-start | bytes 2097152 | tf_op jit(solution)/shard_map/all_to_all | solution.py:15
  133.9 2.2 convolution_bitcast_fusion
  136.0 1.1 copy.149
  137.1 10.2 %all-to-all-done.7 = f32[8,128,2,128]{3,1,2,0:T(8,128)} async-done(((f32[8,128,2,128]{3,1,2,0:T(8,128)}), f32[8,128,2,128]{3,1,2,0:T(8,128)}, u32[]{:S(2)}, u32[]{:S(2)}) %all-to-all-start.7) | async-done | bytes 1048608 | tf_op jit(solution)/shard_map/all_to_all | solution.py:15
  147.3 5.6 %all-to-all-start.10 = ((f32[8,128,2,128]{3,1,2,0:T(8,128)}), f32[8,128,2,128]{3,1,2,0:T(8,128)}, u32[]{:S(2)}, u32[]{:S(2)}) async-start(f32[8,128,2,128]{3,1,2,0:T(8,128)} %bitcast.141), calls=%async_computation.10 | async-start | bytes 2097152 | tf_op jit(solution)/shard_map/all_to_all | solution.py:15
  152.8 1.9 reduce_sum.85
  154.8 1.5 copy.92
  156.3 9.6 %all-to-all-done.10 = f32[8,128,2,128]{3,1,2,0:T(8,128)} async-done(((f32[8,128,2,128]{3,1,2,0:T(8,128)}), f32[8,128,2,128]{3,1,2,0:T(8,128)}, u32[]{:S(2)}, u32[]{:S(2)}) %all-to-all-start.10) | async-done | bytes 1048608 | tf_op jit(solution)/shard_map/all_to_all | solution.py:15
  165.9 4.6 all-to-all-start.8
  170.5 1.9 reduce_sum.86
  172.4 1.5 copy.97
  173.9 6.5 %all-to-all-done.8 = bf16[128,2,128]{2,1,0:T(2,128)(2,1)} async-done(((bf16[128,2,128]{2,1,0:T(2,128)(2,1)}), bf16[128,2,128]{2,1,0:T(2,128)(2,1)}, u32[]{:S(2)}, u32[]{:S(2)}) %all-to-all-start.8) | async-done | bytes 65568 | tf_op jit(solution)/shard_map/all_to_all | solution.py:78
  180.4 4.6 all-to-all-start.11
  185.0 0.9 copy.93
  185.8 0.7 copy.94
  186.5 8.4 %all-to-all-done.11 = bf16[128,2,128]{2,1,0:T(2,128)(2,1)} async-done(((bf16[128,2,128]{2,1,0:T(2,128)(2,1)}), bf16[128,2,128]{2,1,0:T(2,128)(2,1)}, u32[]{:S(2)}, u32[]{:S(2)}) %all-to-all-start.11) | async-done | bytes 65568 | tf_op jit(solution)/shard_map/all_to_all | solution.py:78
  194.9 1.8 broadcast_in_dim.26
  196.7 5.5 %all-to-all-start.9 = ((bf16[8,4,64,128]{3,2,1,0:T(8,128)(2,1)}), bf16[8,4,64,128]{3,2,1,0:T(8,128)(2,1)}, u32[]{:S(2)}, u32[]{:S(2)}) async-start(bf16[8,4,64,128]{3,2,1,0:T(8,128)(2,1)} %broadcast_in_dim.26), calls=%async_computation.9 | async-start | bytes 1048576 | tf_op jit(solution)/shard_map/all_to_all | solution.py:21
  202.1 2.1 convolution_convert_fusion.1
  204.2 3.1 convolution_convert_fusion
  207.3 0.8 copy.98
  208.3 2.6 all-to-all-done.9
  210.8 0.9 broadcast_in_dim.28
  211.8 5.5 %all-to-all-start.12 = ((bf16[8,4,64,128]{3,2,1,0:T(8,128)(2,1)}), bf16[8,4,64,128]{3,2,1,0:T(8,128)(2,1)}, u32[]{:S(2)}, u32[]{:S(2)}) async-start(bf16[8,4,64,128]{3,2,1,0:T(8,128)(2,1)} %broadcast_in_dim.28), calls=%async_computation.12 | async-start | bytes 1048576 | tf_op jit(solution)/shard_map/all_to_all | solution.py:21
  217.2 2.2 multiply_reduce_fusion.1
  219.4 0.7 reshape.65
  220.1 1.5 fusion.19
  221.6 3.5 all-to-all-done.12
  225.2 4.7 all-to-all-start.13
  229.9 2.2 convolution_bitcast_fusion.8
  232.1 2.5 all-to-all-done.13
  234.6 1.2 reduce.1
  235.8 0.8 reshape.66
  237.2 2.5 convolution_bitcast_fusion.6
  239.7 2.5 fusion.2
  242.2 245.3 %all-reduce.2.cloned.1.call-done = f32[1024,64]{0,1:T(8,128)} async-done(((f32[1024,64]{0,1:T(8,128)}), f32[1024,64]{0,1:T(8,128)}) %all-reduce.2.cloned.1.call-update) | async-done | bytes 262160 | tf_op jit(solution)/shard_map/psum | solution.py:144
  487.5 1.7 copy.154
  (32 shorter events, 2.9 us)
Async XLA Ops:
  7.2 108.6 %copy-start = (bf16[2,1024,512]{2,1,0:T(8,128)(2,1)S(1)}, bf16[2,1024,512]{2,1,0:T(8,128)(2,1)}, u32[]{:S(2)}) copy-start(bf16[2,1024,512]{2,1,0:T(8,128)(2,1)} %param.8) | copy-start | bytes 6291460
  20.9 199.2 %copy-start.2 = (f32[4,64]{1,0:T(4,128)}, f32[4,64]{1,0:T(4,128)S(1)}, u32[]{:S(2)}) copy-start(f32[4,64]{1,0:T(4,128)S(1)} %get-tuple-element.10) | copy-start | bytes 3076
  20.9 199.2 %copy-start.3 = (f32[4,64]{1,0:T(4,128)}, f32[4,64]{1,0:T(4,128)S(1)}, u32[]{:S(2)}) copy-start(f32[4,64]{1,0:T(4,128)S(1)} %get-tuple-element.11) | copy-start | bytes 3076
  23.4 18.7 %all-to-all-start.4 = ((f32[8,4,64,128]{3,2,1,0:T(8,128)}), f32[8,4,64,128]{3,2,1,0:T(8,128)}, u32[]{:S(2)}, u32[]{:S(2)}) async-start(f32[8,4,64,128]{3,2,1,0:T(8,128)} %bitcast.137), calls=%async_computation.4 | async-start | bytes 2097152 | tf_op jit(solution)/shard_map/all_to_all | solution.py:15
  29.7 12.4 %copy-start.4 = (f32[4,72]{1,0:T(4,128)}, f32[4,72]{1,0:T(4,128)S(1)}, u32[]{:S(2)}) copy-start(f32[4,72]{1,0:T(4,128)S(1)} %get-tuple-element.14) | copy-start | bytes 3460
  42.1 18.0 %all-to-all-start.1 = ((f32[8,4,64,128]{3,2,1,0:T(8,128)}), f32[8,4,64,128]{3,2,1,0:T(8,128)S(1)}, u32[]{:S(2)}, u32[]{:S(2)}) async-start(f32[8,4,64,128]{3,2,1,0:T(8,128)} %bitcast.140), calls=%async_computation.1 | async-start | bytes 2097152 | tf_op jit(solution)/shard_map/all_to_all | solution.py:15
  60.1 21.2 %all-to-all-start.5 = ((bf16[4,64,128]{2,0,1:T(4,128)(2,1)}), bf16[4,64,128]{2,0,1:T(4,128)(2,1)S(1)}, u32[]{:S(2)}, u32[]{:S(2)}) async-start(bf16[4,64,128]{2,0,1:T(4,128)(2,1)} %copy.87), calls=%async_computation.5 | async-start | bytes 131072 | tf_op jit(solution)/shard_map/all_to_all | solution.py:71
  81.2 13.8 %all-to-all-start.2 = ((bf16[4,64,128]{2,0,1:T(4,128)(2,1)}), bf16[4,64,128]{2,0,1:T(4,128)(2,1)S(1)}, u32[]{:S(2)}, u32[]{:S(2)}) async-start(bf16[4,64,128]{2,0,1:T(4,128)(2,1)} %copy.82), calls=%async_computation.2 | async-start | bytes 131072 | tf_op jit(solution)/shard_map/all_to_all | solution.py:71
  95.9 13.5 %all-to-all-start.6 = ((bf16[8,128,2,128]{3,1,2,0:T(8,128)(2,1)}), bf16[8,128,2,128]{3,1,2,0:T(8,128)(2,1)S(1)}, u32[]{:S(2)}, u32[]{:S(2)}) async-start(bf16[8,128,2,128]{3,1,2,0:T(8,128)(2,1)} %broadcast_in_dim.24), calls=%async_computation.6 | async-start | bytes 1048576 | tf_op jit(solution)/shard_map/all_to_all | solution.py:21
  110.3 13.4 %all-to-all-start.3 = ((bf16[8,128,2,128]{3,1,2,0:T(8,128)(2,1)}), bf16[8,128,2,128]{3,1,2,0:T(8,128)(2,1)}, u32[]{:S(2)}, u32[]{:S(2)}) async-start(bf16[8,128,2,128]{3,1,2,0:T(8,128)(2,1)} %broadcast_in_dim.22), calls=%async_computation.3 | async-start | bytes 1048576 | tf_op jit(solution)/shard_map/all_to_all | solution.py:21
  128.3 18.9 %all-to-all-start.7 = ((f32[8,128,2,128]{3,1,2,0:T(8,128)}), f32[8,128,2,128]{3,1,2,0:T(8,128)}, u32[]{:S(2)}, u32[]{:S(2)}) async-start(f32[8,128,2,128]{3,1,2,0:T(8,128)} %bitcast.142), calls=%async_computation.7 | async-start | bytes 2097152 | tf_op jit(solution)/shard_map/all_to_all | solution.py:15
  147.3 18.6 %all-to-all-start.10 = ((f32[8,128,2,128]{3,1,2,0:T(8,128)}), f32[8,128,2,128]{3,1,2,0:T(8,128)}, u32[]{:S(2)}, u32[]{:S(2)}) async-start(f32[8,128,2,128]{3,1,2,0:T(8,128)} %bitcast.141), calls=%async_computation.10 | async-start | bytes 2097152 | tf_op jit(solution)/shard_map/all_to_all | solution.py:15
  165.9 14.5 %all-to-all-start.8 = ((bf16[128,2,128]{2,1,0:T(2,128)(2,1)}), bf16[128,2,128]{2,1,0:T(2,128)(2,1)}, u32[]{:S(2)}, u32[]{:S(2)}) async-start(bf16[128,2,128]{2,1,0:T(2,128)(2,1)} %copy.92), calls=%async_computation.8 | async-start | bytes 131072 | tf_op jit(solution)/shard_map/all_to_all | solution.py:78
  180.4 14.5 %all-to-all-start.11 = ((bf16[128,2,128]{2,1,0:T(2,128)(2,1)}), bf16[128,2,128]{2,1,0:T(2,128)(2,1)}, u32[]{:S(2)}, u32[]{:S(2)}) async-start(bf16[128,2,128]{2,1,0:T(2,128)(2,1)} %copy.97), calls=%async_computation.11 | async-start | bytes 131072 | tf_op jit(solution)/shard_map/all_to_all | solution.py:78
  196.7 14.2 %all-to-all-start.9 = ((bf16[8,4,64,128]{3,2,1,0:T(8,128)(2,1)}), bf16[8,4,64,128]{3,2,1,0:T(8,128)(2,1)}, u32[]{:S(2)}, u32[]{:S(2)}) async-start(bf16[8,4,64,128]{3,2,1,0:T(8,128)(2,1)} %broadcast_in_dim.26), calls=%async_computation.9 | async-start | bytes 1048576 | tf_op jit(solution)/shard_map/all_to_all | solution.py:21
  211.8 13.4 %all-to-all-start.12 = ((bf16[8,4,64,128]{3,2,1,0:T(8,128)(2,1)}), bf16[8,4,64,128]{3,2,1,0:T(8,128)(2,1)}, u32[]{:S(2)}, u32[]{:S(2)}) async-start(bf16[8,4,64,128]{3,2,1,0:T(8,128)(2,1)} %broadcast_in_dim.28), calls=%async_computation.12 | async-start | bytes 1048576 | tf_op jit(solution)/shard_map/all_to_all | solution.py:21
  221.6 18.1 %copy-start.1 = (bf16[1024,64]{0,1:T(8,128)(2,1)S(1)}, bf16[1024,64]{0,1:T(8,128)(2,1)}, u32[]{:S(2)}) copy-start(bf16[1024,64]{0,1:T(8,128)(2,1)} %param.7) | copy-start | bytes 393220
  225.2 9.4 %all-to-all-start.13 = ((f32[8,1,256]{2,1,0:T(1,128)}), f32[8,1,256]{2,1,0:T(1,128)S(1)}, u32[]{:S(2)}, u32[]{:S(2)}) async-start(f32[8,1,256]{2,1,0:T(1,128)} %reshape.65), calls=%async_computation.13 | async-start | bytes 16384 | tf_op jit(solution)/shard_map/all_to_all | solution.py:21
  229.9 257.6 %all-reduce.2.cloned.1.call-start = ((), (), s32[]{:S(2)}) async-start(), calls=%async_computation.14 | async-start | bytes 524288 | tf_op jit(solution)/shard_map/psum | solution.py:144
Sparse Core Ops, SparseCore 0:
  239.8 247.6 all-reduce.1
where the time goes:
time: 498 us; the launch traced here: 496 us
  waiting for transfers between devices  345 us (69%)
  starting transfers between devices  71.8 us (14%)
  matrix products  26.7 us (5%)
  local copies, waits for them, and re-layouts  19.7 us (4%)
  between operations  14.3 us (3%)
  blocking collectives  10.4 us (2%)
  other arithmetic  8.52 us (2%)
    psum x1, waiting for transfers between devices, on_device(): grad_router = lax.psum(local_router, ('dp', 'tensor'))  245 us
    all_to_all x4, waiting for transfers between devices, summed_on_arrival(): lax.all_to_all(blocks, axis, split_axis=0, concat_axis=0, tiled=True)  40.8 us
    all_to_all x5, starting transfers between devices, sent_to_all(): lax.all_to_all(jnp.broadcast_to(x[None], (length, *x.shape)), axis, 0, 0,...  26 us
    all_to_all x5, waiting for transfers between devices, sent_to_all(): lax.all_to_all(jnp.broadcast_to(x[None], (length, *x.shape)), axis, 0, 0,...  24.6 us
    all_to_all x4, starting transfers between devices, summed_on_arrival(): lax.all_to_all(blocks, axis, split_axis=0, concat_axis=0, tiled=True)  21.6 us
    all_to_all x2, waiting for transfers between devices, to_experts(): lax.all_to_all(shared_part, 'dp', split_axis=1, concat_axis=0, tiled=True)  19.1 us
    all_to_all x2, starting transfers between devices, to_experts(): lax.all_to_all(shared_part, 'dp', split_axis=1, concat_axis=0, tiled=True)  15.1 us
    all_to_all x2, waiting for transfers between devices, to_images(): lax.all_to_all(shared_part, 'dp', split_axis=0, concat_axis=1, tiled=True)  14.8 us
  transfers between devices with their start and end apart: 14, of which 14 were waited for; matrix products, arithmetic and copies ran while one was open for 7% of the time, Pallas kernels for 0%

commit v1 on v0

--- a/solution.py
+++ b/solution.py
@@ -141,7 +141,8 @@
     )
     grad_tokens = (token_part + router_part).astype(jnp.bfloat16)
     local_router = jnp.einsum("isd,ise->de", tokens, grad_logits, preferred_element_type=wide)
-    grad_router = lax.psum(local_router, ("dp", "tensor"))
+    one_axis = lax.psum(local_router, "dp")
+    grad_router = lax.psum(one_axis, "tensor")
     return (grad_tokens, grad_router, grad_w_in, grad_w_out)
 
 

time: 498 us -> 590 us (1.18)
  waiting for transfers between devices: 345 us -> 446 us
    psum x1 -> x2, waiting for transfers between devices: 245 us -> 339 us  [the longest x1 262 us: on_device(): one_axis = lax.psum(local_router, 'dp')]
  transfers between devices with their start and end apart: 14 -> 15, of which waited for: 14 -> 15; matrix products, arithmetic and copies ran while one was open for 7% -> 5% of each run, Pallas kernels for 0% -> 0%
where the time goes in v1:
time: 590 us; the launch traced here: 587 us
  waiting for transfers between devices  446 us (76%)
  starting transfers between devices  70.5 us (12%)
  matrix products  25.8 us (4%)
  between operations  14.3 us (2%)
  local copies, waits for them, and re-layouts  14.2 us (2%)
  blocking collectives  10.4 us (2%)
  other arithmetic  6.26 us (1%)
    psum x1, waiting for transfers between devices, on_device(): one_axis = lax.psum(local_router, 'dp')  262 us
    psum x1, waiting for transfers between devices, on_device(): grad_router = lax.psum(one_axis, 'tensor')  77.2 us
    all_to_all x4, waiting for transfers between devices, summed_on_arrival(): lax.all_to_all(blocks, axis, split_axis=0, concat_axis=0, tiled=True)  42.3 us
    all_to_all x5, waiting for transfers between devices, sent_to_all(): lax.all_to_all(jnp.broadcast_to(x[None], (length, *x.shape)), axis, 0, 0,...  27.4 us
    all_to_all x5, starting transfers between devices, sent_to_all(): lax.all_to_all(jnp.broadcast_to(x[None], (length, *x.shape)), axis, 0, 0,...  26.1 us
    all_to_all x4, starting transfers between devices, summed_on_arrival(): lax.all_to_all(blocks, axis, split_axis=0, concat_axis=0, tiled=True)  21.5 us
    all_to_all x2, waiting for transfers between devices, to_experts(): lax.all_to_all(shared_part, 'dp', split_axis=1, concat_axis=0, tiled=True)  19.1 us
    all_to_all x2, waiting for transfers between devices, to_images(): lax.all_to_all(shared_part, 'dp', split_axis=0, concat_axis=1, tiled=True)  17.8 us
  transfers between devices with their start and end apart: 15, of which 15 were waited for; matrix products, arithmetic and copies ran while one was open for 5% of the time, Pallas kernels for 0%

profile of v1, /device:TPU:2, one launch (start us, length us, event | category | flops | bytes accessed | tf_op | source)
XLA Modules:
  0.0 587.4 jit_solution(12457951196065443920)
XLA Ops:
  7.2 1.7 fusion.48
  9.2 10.4 %all_to_all.110 = f32[8,1,512]{2,1,0:T(1,128)S(1)} all-to-all(f32[8,1,512]{2,1,0:T(1,128)S(1)} %reshape.63), channel_id=1, replica_groups=mesh['dp'=32,'tensor'=8] {'tensor'}, dimensions={0} | all-to-all | bytes 32768 | tf_op jit(solution)/shard_map/all_to_all | solution.py:21
  19.6 0.6 broadcast.40
  20.2 0.7 reduce
  21.0 1.4 convolution_bitcast_fusion.2
  22.4 1.1 copy.151
  23.5 5.6 all-to-all-start.4
  29.1 0.7 fusion.49
  29.8 1.4 convolution_bitcast_fusion.3
  31.2 1.1 copy.152
  32.3 9.9 %all-to-all-done.4 = f32[8,4,64,128]{3,2,1,0:T(8,128)} async-done(((f32[8,4,64,128]{3,2,1,0:T(8,128)}), f32[8,4,64,128]{3,2,1,0:T(8,128)}, u32[]{:S(2)}, u32[]{:S(2)}) %all-to-all-start.4) | async-done | bytes 1048608 | tf_op jit(solution)/shard_map/all_to_all | solution.py:15
  42.2 4.9 all-to-all-start.1
  47.1 1.3 reduce_sum.84
  48.4 0.7 copy.87
  49.1 11.1 %all-to-all-done.1 = f32[8,4,64,128]{3,2,1,0:T(8,128)S(1)} async-done(((f32[8,4,64,128]{3,2,1,0:T(8,128)}), f32[8,4,64,128]{3,2,1,0:T(8,128)S(1)}, u32[]{:S(2)}, u32[]{:S(2)}) %all-to-all-start.1) | async-done | bytes 1048608 | tf_op jit(solution)/shard_map/all_to_all | solution.py:15
  60.2 11.2 %all-to-all-start.5 = ((bf16[4,64,128]{2,0,1:T(4,128)(2,1)}), bf16[4,64,128]{2,0,1:T(4,128)(2,1)S(1)}, u32[]{:S(2)}, u32[]{:S(2)}) async-start(bf16[4,64,128]{2,0,1:T(4,128)(2,1)} %copy.87), calls=%async_computation.5 | async-start | bytes 131072 | tf_op jit(solution)/shard_map/all_to_all | solution.py:71
  71.5 0.7 copy.82
  72.2 9.2 %all-to-all-done.5 = bf16[4,64,128]{2,0,1:T(4,128)(2,1)S(1)} async-done(((bf16[4,64,128]{2,0,1:T(4,128)(2,1)}), bf16[4,64,128]{2,0,1:T(4,128)(2,1)S(1)}, u32[]{:S(2)}, u32[]{:S(2)}) %all-to-all-start.5) | async-done | bytes 65568 | tf_op jit(solution)/shard_map/all_to_all | solution.py:71
  81.4 3.9 all-to-all-start.2
  85.3 9.9 %all-to-all-done.2 = bf16[4,64,128]{2,0,1:T(4,128)(2,1)S(1)} async-done(((bf16[4,64,128]{2,0,1:T(4,128)(2,1)}), bf16[4,64,128]{2,0,1:T(4,128)(2,1)S(1)}, u32[]{:S(2)}, u32[]{:S(2)}) %all-to-all-start.2) | async-done | bytes 65568 | tf_op jit(solution)/shard_map/all_to_all | solution.py:71
  95.2 0.9 broadcast_in_dim.24
  96.1 4.9 all-to-all-start.6
  101.0 8.5 %all-to-all-done.6 = bf16[8,128,2,128]{3,1,2,0:T(8,128)(2,1)S(1)} async-done(((bf16[8,128,2,128]{3,1,2,0:T(8,128)(2,1)}), bf16[8,128,2,128]{3,1,2,0:T(8,128)(2,1)S(1)}, u32[]{:S(2)}, u32[]{:S(2)}) %all-to-all-start.6) | async-done | bytes 524320 | tf_op jit(solution)/shard_map/all_to_all | solution.py:21
  109.5 0.9 broadcast_in_dim.22
  110.4 5.5 all-to-all-start.3
  115.9 0.5 convolution_bitcast_fusion.4
  116.4 7.5 %all-to-all-done.3 = bf16[8,128,2,128]{3,1,2,0:T(8,128)(2,1)} async-done(((bf16[8,128,2,128]{3,1,2,0:T(8,128)(2,1)}), bf16[8,128,2,128]{3,1,2,0:T(8,128)(2,1)}, u32[]{:S(2)}, u32[]{:S(2)}) %all-to-all-start.3) | async-done | bytes 524320 | tf_op jit(solution)/shard_map/all_to_all | solution.py:21
  123.8 2.8 fusion.15
  126.6 0.8 convolution_bitcast_fusion.1
  127.4 1.1 copy.150
  128.5 5.5 all-to-all-start.7
  134.0 2.2 convolution_bitcast_fusion
  136.2 1.1 copy.149
  137.2 10.2 %all-to-all-done.7 = f32[8,128,2,128]{3,1,2,0:T(8,128)} async-done(((f32[8,128,2,128]{3,1,2,0:T(8,128)}), f32[8,128,2,128]{3,1,2,0:T(8,128)}, u32[]{:S(2)}, u32[]{:S(2)}) %all-to-all-start.7) | async-done | bytes 1048608 | tf_op jit(solution)/shard_map/all_to_all | solution.py:15
  147.4 5.6 all-to-all-start.10
  153.0 1.3 reduce_sum.85
  154.3 0.7 copy.92
  155.0 11.1 %all-to-all-done.10 = f32[8,128,2,128]{3,1,2,0:T(8,128)} async-done(((f32[8,128,2,128]{3,1,2,0:T(8,128)}), f32[8,128,2,128]{3,1,2,0:T(8,128)}, u32[]{:S(2)}, u32[]{:S(2)}) %all-to-all-start.10) | async-done | bytes 1048608 | tf_op jit(solution)/shard_map/all_to_all | solution.py:15
  166.0 3.9 all-to-all-start.8
  169.9 1.3 reduce_sum.86
  171.2 0.7 copy.97
  171.9 8.0 %all-to-all-done.8 = bf16[128,2,128]{2,1,0:T(2,128)(2,1)S(1)} async-done(((bf16[128,2,128]{2,1,0:T(2,128)(2,1)}), bf16[128,2,128]{2,1,0:T(2,128)(2,1)S(1)}, u32[]{:S(2)}, u32[]{:S(2)}) %all-to-all-start.8) | async-done | bytes 65568 | tf_op jit(solution)/shard_map/all_to_all | solution.py:78
  179.8 3.9 all-to-all-start.11
  183.8 9.9 %all-to-all-done.11 = bf16[128,2,128]{2,1,0:T(2,128)(2,1)S(1)} async-done(((bf16[128,2,128]{2,1,0:T(2,128)(2,1)}), bf16[128,2,128]{2,1,0:T(2,128)(2,1)S(1)}, u32[]{:S(2)}, u32[]{:S(2)}) %all-to-all-start.11) | async-done | bytes 65568 | tf_op jit(solution)/shard_map/all_to_all | solution.py:78
  193.7 0.9 broadcast_in_dim.26
  194.6 5.5 all-to-all-start.9
  200.0 3.1 convolution_convert_fusion
  203.3 5.5 all-to-all-done.9
  208.8 0.9 broadcast_in_dim.28
  209.7 5.6 all-to-all-start.12
  215.3 3.0 convolution_convert_fusion.1
  218.3 1.4 multiply_reduce_fusion.1
  219.8 0.7 reshape.65
  220.4 2.8 all-to-all-done.12
  223.2 4.7 all-to-all-start.13
  227.9 1.5 convolution_bitcast_fusion.8
  229.5 3.2 all-to-all-done.13
  232.6 0.7 reduce.1
  233.4 2.1 convolution_bitcast_fusion.6
  235.6 1.5 fusion.19
  237.1 262.0 %all-reduce.3.cloned.1.call-done = f32[1024,64]{0,1:T(8,128)} async-done(((f32[1024,64]{0,1:T(8,128)}), f32[1024,64]{0,1:T(8,128)}) %all-reduce.3.cloned.1.call-update) | async-done | bytes 262160 | tf_op jit(solution)/shard_map/psum | solution.py:144
  499.2 2.4 fusion.2
  501.7 77.2 %all-reduce.5.cloned.1.call-done = f32[1024,64]{0,1:T(8,128)} async-done(((f32[1024,64]{0,1:T(8,128)}), f32[1024,64]{0,1:T(8,128)}) %all-reduce.5.cloned.1.call-update) | async-done | bytes 262160 | tf_op jit(solution)/shard_map/psum | solution.py:145
  578.9 1.7 copy.155
  (37 shorter events, 1.0 us)
Async XLA Ops:
  7.2 108.8 %copy-start = (bf16[2,1024,512]{2,1,0:T(8,128)(2,1)S(1)}, bf16[2,1024,512]{2,1,0:T(8,128)(2,1)}, u32[]{:S(2)}) copy-start(bf16[2,1024,512]{2,1,0:T(8,128)(2,1)} %param.8) | copy-start | bytes 6291460
  23.5 18.7 %all-to-all-start.4 = ((f32[8,4,64,128]{3,2,1,0:T(8,128)}), f32[8,4,64,128]{3,2,1,0:T(8,128)}, u32[]{:S(2)}, u32[]{:S(2)}) async-start(f32[8,4,64,128]{3,2,1,0:T(8,128)} %bitcast.137), calls=%async_computation.4 | async-start | bytes 2097152 | tf_op jit(solution)/shard_map/all_to_all | solution.py:15
  42.2 18.0 %all-to-all-start.1 = ((f32[8,4,64,128]{3,2,1,0:T(8,128)}), f32[8,4,64,128]{3,2,1,0:T(8,128)S(1)}, u32[]{:S(2)}, u32[]{:S(2)}) async-start(f32[8,4,64,128]{3,2,1,0:T(8,128)} %bitcast.140), calls=%async_computation.1 | async-start | bytes 2097152 | tf_op jit(solution)/shard_map/all_to_all | solution.py:15
  60.2 21.2 %all-to-all-start.5 = ((bf16[4,64,128]{2,0,1:T(4,128)(2,1)}), bf16[4,64,128]{2,0,1:T(4,128)(2,1)S(1)}, u32[]{:S(2)}, u32[]{:S(2)}) async-start(bf16[4,64,128]{2,0,1:T(4,128)(2,1)} %copy.87), calls=%async_computation.5 | async-start | bytes 131072 | tf_op jit(solution)/shard_map/all_to_all | solution.py:71
  81.4 13.8 %all-to-all-start.2 = ((bf16[4,64,128]{2,0,1:T(4,128)(2,1)}), bf16[4,64,128]{2,0,1:T(4,128)(2,1)S(1)}, u32[]{:S(2)}, u32[]{:S(2)}) async-start(bf16[4,64,128]{2,0,1:T(4,128)(2,1)} %copy.82), calls=%async_computation.2 | async-start | bytes 131072 | tf_op jit(solution)/shard_map/all_to_all | solution.py:71
  96.1 13.5 %all-to-all-start.6 = ((bf16[8,128,2,128]{3,1,2,0:T(8,128)(2,1)}), bf16[8,128,2,128]{3,1,2,0:T(8,128)(2,1)S(1)}, u32[]{:S(2)}, u32[]{:S(2)}) async-start(bf16[8,128,2,128]{3,1,2,0:T(8,128)(2,1)} %broadcast_in_dim.24), calls=%async_computation.6 | async-start | bytes 1048576 | tf_op jit(solution)/shard_map/all_to_all | solution.py:21
  110.4 13.4 %all-to-all-start.3 = ((bf16[8,128,2,128]{3,1,2,0:T(8,128)(2,1)}), bf16[8,128,2,128]{3,1,2,0:T(8,128)(2,1)}, u32[]{:S(2)}, u32[]{:S(2)}) async-start(bf16[8,128,2,128]{3,1,2,0:T(8,128)(2,1)} %broadcast_in_dim.22), calls=%async_computation.3 | async-start | bytes 1048576 | tf_op jit(solution)/shard_map/all_to_all | solution.py:21
  126.6 1.9 copy-start.2
  128.5 18.9 %all-to-all-start.7 = ((f32[8,128,2,128]{3,1,2,0:T(8,128)}), f32[8,128,2,128]{3,1,2,0:T(8,128)}, u32[]{:S(2)}, u32[]{:S(2)}) async-start(f32[8,128,2,128]{3,1,2,0:T(8,128)} %bitcast.142), calls=%async_computation.7 | async-start | bytes 2097152 | tf_op jit(solution)/shard_map/all_to_all | solution.py:15
  147.4 18.6 %all-to-all-start.10 = ((f32[8,128,2,128]{3,1,2,0:T(8,128)}), f32[8,128,2,128]{3,1,2,0:T(8,128)}, u32[]{:S(2)}, u32[]{:S(2)}) async-start(f32[8,128,2,128]{3,1,2,0:T(8,128)} %bitcast.141), calls=%async_computation.10 | async-start | bytes 2097152 | tf_op jit(solution)/shard_map/all_to_all | solution.py:15
  166.0 13.8 %all-to-all-start.8 = ((bf16[128,2,128]{2,1,0:T(2,128)(2,1)}), bf16[128,2,128]{2,1,0:T(2,128)(2,1)S(1)}, u32[]{:S(2)}, u32[]{:S(2)}) async-start(bf16[128,2,128]{2,1,0:T(2,128)(2,1)} %copy.92), calls=%async_computation.8 | async-start | bytes 131072 | tf_op jit(solution)/shard_map/all_to_all | solution.py:78
  179.8 13.8 %all-to-all-start.11 = ((bf16[128,2,128]{2,1,0:T(2,128)(2,1)}), bf16[128,2,128]{2,1,0:T(2,128)(2,1)S(1)}, u32[]{:S(2)}, u32[]{:S(2)}) async-start(bf16[128,2,128]{2,1,0:T(2,128)(2,1)} %copy.97), calls=%async_computation.11 | async-start | bytes 131072 | tf_op jit(solution)/shard_map/all_to_all | solution.py:78
  194.6 14.2 %all-to-all-start.9 = ((bf16[8,4,64,128]{3,2,1,0:T(8,128)(2,1)}), bf16[8,4,64,128]{3,2,1,0:T(8,128)(2,1)}, u32[]{:S(2)}, u32[]{:S(2)}) async-start(bf16[8,4,64,128]{3,2,1,0:T(8,128)(2,1)} %broadcast_in_dim.26), calls=%async_computation.9 | async-start | bytes 1048576 | tf_op jit(solution)/shard_map/all_to_all | solution.py:21
  209.7 8.6 %copy-start.1 = (bf16[4,72,1024]{2,1,0:T(8,128)(2,1)S(1)}, bf16[4,72,1024]{2,1,0:T(8,128)(2,1)}, u32[]{:S(2)}) copy-start(bf16[4,72,1024]{2,1,0:T(8,128)(2,1)} %param.5) | copy-start | bytes 1769476
  209.7 13.5 %all-to-all-start.12 = ((bf16[8,4,64,128]{3,2,1,0:T(8,128)(2,1)}), bf16[8,4,64,128]{3,2,1,0:T(8,128)(2,1)}, u32[]{:S(2)}, u32[]{:S(2)}) async-start(bf16[8,4,64,128]{3,2,1,0:T(8,128)(2,1)} %broadcast_in_dim.28), calls=%async_computation.12 | async-start | bytes 1048576 | tf_op jit(solution)/shard_map/all_to_all | solution.py:21
  219.7 15.8 %copy-start.4 = (f32[4,72,64]{1,2,0:T(8,128)}, f32[4,72,64]{1,2,0:T(8,128)S(1)}, u32[]{:S(2)}) copy-start(f32[4,72,64]{1,2,0:T(8,128)S(1)} %get-tuple-element.17) | copy-start | bytes 221188
  223.2 9.4 %all-to-all-start.13 = ((f32[8,1,256]{2,1,0:T(1,128)}), f32[8,1,256]{2,1,0:T(1,128)S(1)}, u32[]{:S(2)}, u32[]{:S(2)}) async-start(f32[8,1,256]{2,1,0:T(1,128)} %reshape.65), calls=%async_computation.13 | async-start | bytes 16384 | tf_op jit(solution)/shard_map/all_to_all | solution.py:21
  227.9 271.3 %all-reduce.3.cloned.1.call-start = ((), (), s32[]{:S(2)}) async-start(), calls=%async_computation.14 | async-start | bytes 524288 | tf_op jit(solution)/shard_map/psum | solution.py:144
  229.4 6.1 %copy-start.5 = (f32[4,72,64]{1,2,0:T(8,128)}, f32[4,72,64]{1,2,0:T(8,128)S(1)}, u32[]{:S(2)}) copy-start(f32[4,72,64]{1,2,0:T(8,128)S(1)} %convolution_bitcast_fusion.8) | copy-start | bytes 221188
  229.5 269.8 %copy-start.3 = (bf16[1024,64]{0,1:T(8,128)(2,1)S(1)}, bf16[1024,64]{0,1:T(8,128)(2,1)}, u32[]{:S(2)}) copy-start(bf16[1024,64]{0,1:T(8,128)(2,1)} %param.7) | copy-start | bytes 393220
  235.6 343.3 %all-reduce.5.cloned.1.call-start = ((), (), s32[]{:S(2)}) async-start(), calls=%async_computation.15 | async-start | bytes 524288 | tf_op jit(solution)/shard_map/psum | solution.py:145
Sparse Core Ops, SparseCore 0:
  235.7 263.4 all-reduce.2
  501.8 77.0 all-reduce.4
